TPU v7x, 32 devices: a whole 2x2x4 slice. The times are simulated.
32 devices in a mesh: dp: 8 (over y, x, core), mp: 4 (over z).
Axes of the slice: x: 2, y: 2, z: 4, core: 2. Of those that a mesh axis runs over, the one named last changes fastest.
Arguments:
- patches: bfloat16 [192, 64, 1024], P(('dp', 'mp')), may hold values from -6 to 6
- gain_first: float32 [1024], replicated, may hold values from 0.1 to 1.9
- joint_weight: bfloat16 [1024, 3, 1024], P('dp', None, 'mp'), may hold values from -0.1875 to 0.1875
- head_scale: float32 [16], P('mp'), may hold values from 2 to 32
- output_weight: bfloat16 [1024, 1024], P('mp', 'dp'), may hold values from -0.1875 to 0.1875
- gain_second: float32 [1024], replicated, may hold values from 0.3 to 3
- up_weight: bfloat16 [1024, 4096], P('dp', 'mp'), may hold values from -0.1875 to 0.1875
- down_weight: bfloat16 [4096, 1024], P('mp', 'dp'), may hold values from -0.09375 to 0.09375
- gain_final: float32 [1024], replicated, may hold values from 0.1 to 1.9
- project_weight: bfloat16 [1024, 768], replicated, may hold values from -0.1875 to 0.1875
- text_bank: bfloat16 [3072, 768], P(('dp', 'mp')), may hold values from -20000 to 20000
- captions: int32 [192], replicated, may hold values from 0 to 3071
- reference_loss: float32 [192], P(('dp', 'mp')), may hold values from 2 to 20
Outputs:
- learnability: float32 [192], P(('dp', 'mp'))
All inputs are finite; a program needn't handle non-finite values.
Results may differ from a plain program's by a relative error of at most 0.018.
Values may be sent and summed in bfloat16 or wider, within the bound.
A program may use at most 128 MiB of HBM per device.

v0:
```python
import jax
import jax.numpy as jnp
from jax import lax
from jax.sharding import PartitionSpec as P


def layer_norm(values, gain):
    centre = values - jnp.mean(values, axis=-1, keepdims=True)
    spread = jnp.mean(centre * centre, axis=-1, keepdims=True)
    return centre * lax.rsqrt(spread + 1e-06) * gain


def unit_rows(values):
    return values * lax.rsqrt(jnp.sum(values * values, axis=-1, keepdims=True) + 1e-06)


def gather_images(values):
    return lax.all_gather(values, "mp", axis=0, tiled=True)


def group_sums(term):
    return lax.psum_scatter(
        term.astype(jnp.bfloat16), "mp", scatter_dimension=0, tiled=True
    ).astype(jnp.float32)


def attend(normed_rows, joint_full, scales, image_count, patch_count):
    features = normed_rows.shape[1]
    local_heads = scales.shape[0]
    head_width = joint_full.shape[2] // local_heads
    joint = jnp.dot(
        normed_rows, joint_full.reshape(features, -1), preferred_element_type=jnp.float32
    )
    joint = joint.reshape(image_count, patch_count, 3, local_heads, head_width)
    queries = unit_rows(joint[:, :, 0]).astype(jnp.bfloat16)
    key_rows = unit_rows(joint[:, :, 1]).astype(jnp.bfloat16)
    value_rows = joint[:, :, 2].astype(jnp.bfloat16)
    scores = jnp.einsum("bqhd,bkhd->bhqk", queries, key_rows, preferred_element_type=jnp.float32)
    exponent = jnp.exp(scores * scales[None, :, None, None])
    attention = (exponent / jnp.sum(exponent, axis=-1, keepdims=True)).astype(jnp.bfloat16)
    head_out = jnp.einsum(
        "bhqk,bkhd->bqhd", attention, value_rows, preferred_element_type=jnp.float32
    ).astype(jnp.bfloat16)
    return head_out.reshape(image_count * patch_count, local_heads * head_width)


def shards(
    patches,
    gain_first,
    joint_weight,
    head_scale,
    output_weight,
    gain_second,
    up_weight,
    down_weight,
    gain_final,
    project_weight,
    text_bank,
    captions,
    reference_loss,
):
    joint_full, output_full, up_full, down_full = (
        lax.all_gather(joint_weight, "dp", axis=0, tiled=True),
        lax.all_gather(output_weight, "dp", axis=1, tiled=True),
        lax.all_gather(up_weight, "dp", axis=0, tiled=True),
        lax.all_gather(down_weight, "dp", axis=1, tiled=True),
    )
    own_images, patch_count, features = patches.shape
    residual = patches.astype(jnp.float32)
    normed_first = layer_norm(residual, gain_first).astype(jnp.bfloat16)
    group_images = own_images * lax.axis_size("mp")
    gathered = gather_images(normed_first).reshape(group_images * patch_count, features)
    head_out = attend(gathered, joint_full, head_scale, group_images, patch_count)
    mixing_term = jnp.dot(head_out, output_full, preferred_element_type=jnp.float32)
    residual_two = residual + group_sums(mixing_term.reshape(group_images, patch_count, features))
    normed_second = layer_norm(residual_two, gain_second).astype(jnp.bfloat16)
    gathered_two = gather_images(normed_second).reshape(group_images * patch_count, features)
    upper = jnp.dot(gathered_two, up_full, preferred_element_type=jnp.float32)
    hidden = jax.nn.gelu(upper, approximate=False).astype(jnp.bfloat16)
    down_term = jnp.dot(hidden, down_full, preferred_element_type=jnp.float32).reshape(
        group_images, patch_count, features
    )
    feed = group_sums(down_term)
    pooled = jnp.sum(residual_two + feed, axis=1) / patch_count
    pooled_norm = layer_norm(pooled, gain_final).astype(jnp.bfloat16)
    embedded = jnp.dot(pooled_norm, project_weight, preferred_element_type=jnp.float32)
    image_units = unit_rows(embedded).astype(jnp.bfloat16)
    first_row = lax.axis_index(("dp", "mp")) * own_images
    own_captions = lax.dynamic_slice_in_dim(captions, first_row, own_images)
    highest = jnp.full((own_images,), -1e30, jnp.float32)
    logits = lax.dot_general(
        image_units,
        lax.all_gather(text_bank, ("dp", "mp"), axis=0, tiled=True),
        (((1,), (1,)), ((), ())),
        preferred_element_type=jnp.float32,
    )
    new_highest = jnp.maximum(highest, jnp.max(logits, axis=1))
    totals = jnp.sum(jnp.exp(logits - new_highest[:, None]), axis=1)
    text_ids = lax.broadcasted_iota(jnp.int32, logits.shape, 1)
    matched = jnp.sum(jnp.where(text_ids == own_captions[:, None], logits, 0.0), axis=1)
    highest, totals, matched = (new_highest, totals, matched)
    return highest + jnp.log(totals) - matched - reference_loss


def solution(mesh):
    placed = (
        P(("dp", "mp"), None, None),
        P(),
        P("dp", None, "mp"),
        P("mp"),
        P("mp", "dp"),
        P(),
        P("dp", "mp"),
        P("mp", "dp"),
        P(),
        P(),
        P(("dp", "mp"), None),
        P(),
        P(("dp", "mp")),
    )
    return jax.shard_map(
        shards, mesh=mesh, in_specs=placed, out_specs=P(("dp", "mp")), check_vma=False
    )
```

profile of v0, /device:TPU:0, one launch (start us, length us, event | category | flops | bytes accessed | tf_op | source)
XLA Modules:
  0.0 441.4 jit_solution(5458300674794012667)
XLA Ops:
  7.4 1.9 copy.28
  9.3 0.0 all-gather.9.cloned.1.call-update
  9.3 0.0 all-gather.7.cloned.1.call-start
  9.3 1.3 convert_reduce_fusion
  10.7 1.5 fusion.16
  12.1 2.3 fusion.18
  14.5 0.0 all-gather.7.cloned.1.call-update
  14.5 0.0 reduce-scatter.3.cloned.1.call-start
  14.6 12.7 %all_gather.23 = bf16[256,1024]{1,0:T(8,128)(2,1)S(1)} all-gather(bf16[256,128]{1,0:T(8,128)(2,1)S(1)} %copy-done.3), channel_id=1, replica_groups=mesh['dp'=8,'mp'=4] {'dp'}, dimensions={1}, use_global_device_ids=true | all-gather | bytes 589824 | tf_op jit(solution)/shard_map/all_gather | solution.py:64
  27.2 12.6 %all-gather.9.cloned.1.call-done = bf16[1024,3,256]{0,2,1:T(8,128)(2,1)} async-done(((bf16[128,3,256]{0,2,1:T(8,128)(2,1)}), bf16[1024,3,256]{0,2,1:T(8,128)(2,1)}) %all-gather.9.cloned.1.call-update) | async-done | bytes 1572880 | tf_op jit(solution)/shard_map/all_gather | solution.py:63
  39.8 65.0 %all-gather.7.cloned.1.call-done = bf16[24,64,1024]{2,1,0:T(8,128)(2,1)} async-done(((bf16[6,64,1024]{2,1,0:T(8,128)(2,1)}), bf16[24,64,1024]{2,1,0:T(8,128)(2,1)}) %all-gather.7.cloned.1.call-update) | async-done | bytes 3145744 | tf_op jit(solution)/shard_map/all_gather | solution.py:18
  104.9 7.4 %fusion.10 = f32[24,64,3,4,64]{1,4,3,2,0:T(8,128)S(1)} fusion(bf16[3,4,64,1024,1]{3,2,1,0,4:T(8,128)(2,1)} %bitcast.51, bf16[24,64,1024]{2,1,0:T(8,128)(2,1)} %all-gather.7.cloned.1.call-done), kind=kOutput, calls=%fused_computation.23 | convolution fusion | flops 2415919104 | bytes 9437184 | tf_op jit(solution)/shard_map/dot_general | solution.py:31
  112.3 0.0 copy-start.6
  112.3 1.3 multiply_reduce_fusion.1
  113.6 1.2 fusion.13
  114.9 0.9 convolution_convert_fusion.2
  115.7 2.7 convolution_convert_fusion.1
  118.4 0.0 reduce-scatter.3.cloned.1.call-update
  118.5 0.0 all-gather.13.cloned.1.call-start
  118.5 0.5 all-gather.13.cloned.1.call-update
  119.0 0.0 all-gather.15.cloned.1.call-start
  119.1 0.5 all-gather.15.cloned.1.call-update
  119.6 0.0 all-gather.11.cloned.1.call-start
  119.7 58.0 %reduce-scatter.3.cloned.1.call-done = bf16[6,64,1024]{2,1,0:T(8,128)(2,1)} async-done(((bf16[24,64,1024]{2,1,0:T(8,128)(2,1)}), bf16[6,64,1024]{2,1,0:T(8,128)(2,1)}) %reduce-scatter.3.cloned.1.call-update) | async-done | bytes 786448 | tf_op jit(solution)/shard_map/reduce_scatter | solution.py:22
  177.7 1.5 fusion.25
  179.2 1.5 multiply_reduce_fusion.2
  180.7 1.2 multiply_convert_fusion.4
  181.9 0.0 all-gather.11.cloned.1.call-update
  182.0 0.2 reduce-scatter.5.cloned.1.call-start
  182.2 24.9 %all-gather.13.cloned.1.call-done = bf16[1024,1024]{1,0:T(8,128)(2,1)} async-done(((bf16[128,1024]{1,0:T(8,128)(2,1)}), bf16[1024,1024]{1,0:T(8,128)(2,1)}) %all-gather.13.cloned.1.call-update) | async-done | bytes 2097168 | tf_op jit(solution)/shard_map/all_gather | solution.py:65
  207.1 29.9 %all-gather.15.cloned.1.call-done = bf16[1024,1024]{1,0:T(8,128)(2,1)} async-done(((bf16[1024,128]{1,0:T(8,128)(2,1)}), bf16[1024,1024]{1,0:T(8,128)(2,1)}) %all-gather.15.cloned.1.call-update) | async-done | bytes 2097168 | tf_op jit(solution)/shard_map/all_gather | solution.py:66
  237.0 64.9 %all-gather.11.cloned.1.call-done = bf16[24,64,1024]{2,1,0:T(8,128)(2,1)} async-done(((bf16[6,64,1024]{2,1,0:T(8,128)(2,1)}), bf16[24,64,1024]{2,1,0:T(8,128)(2,1)}) %all-gather.11.cloned.1.call-update) | async-done | bytes 3145744 | tf_op jit(solution)/shard_map/all_gather | solution.py:18
  301.9 22.5 %convolution_convert_fusion = bf16[1536,1024]{1,0:T(8,128)(2,1)} fusion(bf16[1024,1024]{1,0:T(8,128)(2,1)} %all-gather.15.cloned.1.call-done, bf16[1536,1024]{1,0:T(8,128)(2,1)} %bitcast.50, bf16[1024,1024]{1,0:T(8,128)(2,1)} %all-gather.13.cloned.1.call-done), kind=kOutput, calls=%fused_computation.19 | convolution fusion | flops 6546259968 | bytes 10485760 | tf_op jit(solution)/shard_map/dot_general | solution.py:80
  324.4 0.0 reduce-scatter.5.cloned.1.call-update
  324.4 0.0 all-gather.17.cloned.1.call-start
  324.5 0.5 all-gather.17.cloned.1.call-update
  325.0 0.1 copy-done.8
  325.1 0.1 dynamic_slice.3
  325.1 60.6 %reduce-scatter.5.cloned.1.call-done = bf16[6,64,1024]{2,1,0:T(8,128)(2,1)} async-done(((bf16[24,64,1024]{2,1,0:T(8,128)(2,1)}), bf16[6,64,1024]{2,1,0:T(8,128)(2,1)}) %reduce-scatter.5.cloned.1.call-update) | async-done | bytes 786448 | tf_op jit(solution)/shard_map/reduce_scatter | solution.py:22
  385.7 1.6 add_reduce_fusion
  387.3 0.1 multiply_reduce_fusion.4
  387.4 0.2 multiply_reduce_fusion.3
  387.6 0.0 copy-start.7
  387.6 0.5 multiply_reduce_fusion.5
  388.1 41.3 %all-gather.17.cloned.1.call-done = bf16[3072,768]{1,0:T(8,128)(2,1)} async-done(((bf16[96,768]{1,0:T(8,128)(2,1)}), bf16[3072,768]{1,0:T(8,128)(2,1)}) %all-gather.17.cloned.1.call-update) | async-done | bytes 4718608 | tf_op jit(solution)/shard_map/all_gather | solution.py:93
  429.4 3.8 fusion.65
  433.2 0.2 exponential_reduce_fusion
  433.5 0.5 subtract_subtract_fusion
  (25 shorter events, 0.1 us)
Async XLA Ops:
  7.4 380.3 %copy-start = (bf16[1024,768]{1,0:T(8,128)(2,1)S(1)}, bf16[1024,768]{1,0:T(8,128)(2,1)}, u32[]{:S(2)}) copy-start(bf16[1024,768]{1,0:T(8,128)(2,1)} %param.22) | copy-start | bytes 4718596
  7.4 7.2 %copy-start.3 = (bf16[256,128]{1,0:T(8,128)(2,1)S(1)}, bf16[256,128]{1,0:T(8,128)(2,1)}, u32[]{:S(2)}) copy-start(bf16[256,128]{1,0:T(8,128)(2,1)} %param.17) | copy-start | bytes 196612
  7.4 32.5 %all-gather.9.cloned.1.call-start = ((), (), s32[]{:S(2)}) async-start(), calls=%async_computation.3 | async-start | bytes 1769472 | tf_op jit(solution)/shard_map/all_gather | solution.py:63
  9.3 95.6 %all-gather.7.cloned.1.call-start = ((), (), s32[]{:S(2)}) async-start(), calls=%async_computation.2 | async-start | bytes 3932160 | tf_op jit(solution)/shard_map/all_gather | solution.py:18
  14.5 163.2 %reduce-scatter.3.cloned.1.call-start = ((), (), s32[]{:S(2)}) async-start(), calls=%async_computation.4 | async-start | bytes 3932160 | tf_op jit(solution)/shard_map/reduce_scatter | solution.py:22
  112.3 1.3 copy-start.6
  118.4 59.2 %copy-start.1 = (bf16[6,64,1024]{2,1,0:T(8,128)(2,1)S(1)}, bf16[6,64,1024]{2,1,0:T(8,128)(2,1)}, u32[]{:S(2)}) copy-start(bf16[6,64,1024]{2,1,0:T(8,128)(2,1)} %param.13) | copy-start | bytes 2359300
  118.4 62.3 %copy-start.4 = (f32[1024]{0:T(1024)S(1)}, f32[1024]{0:T(1024)}, u32[]{:S(2)}) copy-start(f32[1024]{0:T(1024)} %param.18) | copy-start | bytes 12292
  118.5 88.7 %all-gather.13.cloned.1.call-start = ((), (), s32[]{:S(2)}) async-start(), calls=%async_computation.6 | async-start | bytes 2359296 | tf_op jit(solution)/shard_map/all_gather | solution.py:65
  119.0 117.9 %all-gather.15.cloned.1.call-start = ((), (), s32[]{:S(2)}) async-start(), calls=%async_computation.7 | async-start | bytes 2359296 | tf_op jit(solution)/shard_map/all_gather | solution.py:66
  119.6 182.3 %all-gather.11.cloned.1.call-start = ((), (), s32[]{:S(2)}) async-start(), calls=%async_computation.5 | async-start | bytes 3932160 | tf_op jit(solution)/shard_map/all_gather | solution.py:18
  177.7 3.0 copy-start.2
  182.0 203.8 %reduce-scatter.5.cloned.1.call-start = ((), (), s32[]{:S(2)}) async-start(), calls=%async_computation.8 | async-start | bytes 3932160 | tf_op jit(solution)/shard_map/reduce_scatter | solution.py:22
  324.4 0.7 copy-start.8
  324.4 63.2 %copy-start.5 = (f32[1024]{0:T(1024)S(1)}, f32[1024]{0:T(1024)}, u32[]{:S(2)}) copy-start(f32[1024]{0:T(1024)} %param.21) | copy-start | bytes 12292
  324.4 105.0 %all-gather.17.cloned.1.call-start = ((), (), s32[]{:S(2)}) async-start(), calls=%async_computation.9 | async-start | bytes 4866048 | tf_op jit(solution)/shard_map/all_gather | solution.py:93
  387.6 45.8 %copy-start.7 = (f32[6]{0:T(128)S(1)}, f32[6]{0:T(128)}, u32[]{:S(2)}) copy-start(f32[6]{0:T(128)} %param.25) | copy-start | bytes 76
Sparse Core Ops, SparseCore 0:
  10.0 29.7 all-gather.8
  41.4 63.4 all-gather.6
  118.6 59.0 reduce-scatter.2
  179.4 27.6 all-gather.12
  208.8 28.0 all-gather.14
  238.4 63.4 all-gather.10
  324.5 61.1 reduce-scatter.4
Sparse Core Ops, SparseCore 1:
  327.7 101.7 all-gather.16
where the time goes:
time: 442 us; the launch traced here: 441 us
  waiting for transfers between devices  359 us (81%)
  matrix products  38.9 us (9%)
  between operations  15.1 us (3%)
  other arithmetic  13.3 us (3%)
  blocking collectives  12.7 us (3%)
    all_gather x2, waiting for transfers between devices, gather_images(): return lax.all_gather(values, 'mp', axis=0, tiled=True)  130 us
    reduce_scatter x2, waiting for transfers between devices, group_sums(): lax.psum_scatter(term.astype(jnp.bfloat16), 'mp', scatter_dimension=0, ti...  119 us
    all_gather x1, waiting for transfers between devices, shards(): lax.all_gather(text_bank, ('dp', 'mp'), axis=0, tiled=True)  41.3 us
    all_gather x1, waiting for transfers between devices, shards(): lax.all_gather(down_weight, 'dp', axis=1, tiled=True)  29.9 us
    all_gather x1, waiting for transfers between devices, shards(): lax.all_gather(up_weight, 'dp', axis=0, tiled=True)  24.9 us
    dot_general x1, matrix products, shards(): jnp.dot(hidden, down_full, preferred_element_type=jnp.float32)  22.5 us
    all_gather x1, blocking collectives, shards(): lax.all_gather(output_weight, 'dp', axis=1, tiled=True)  12.7 us
    all_gather x1, waiting for transfers between devices, shards(): lax.all_gather(joint_weight, 'dp', axis=0, tiled=True)  12.6 us
  transfers between devices with their start and end apart: 8, of which 8 were waited for; matrix products, arithmetic and copies ran while one was open for 3% of the time, Pallas kernels for 0%

commit v1 on v0

v1 whole, which is shorter than its diff:
```python
import functools

import jax
import jax.numpy as jnp
from jax import lax
from jax.experimental import pallas as pl
from jax.experimental.pallas import tpu as pltpu
from jax.sharding import PartitionSpec as P

MESH = pl.DeviceIdType.MESH
Z, X, Y, D0, D1, S_COL, S_X, S_Y, S_D0, S_D1 = range(10)
KINDS = 10


def flip(index, bit):
    return index + bit - 2 * bit * ((index // bit) % 2)


def gather_kernel(n_mp, own_ref, full_ref, send_sem, recv_sem, local_sem):
    parts, rows, _ = own_ref.shape
    dp, mp = lax.axis_index("dp"), lax.axis_index("mp")
    sib, xn, yn = flip(dp, 1), flip(dp, 2), flip(dp, 4)
    dn = flip(xn, 4)
    right, left = lax.rem(mp + 1, n_mp), lax.rem(mp + n_mp - 1, n_mp)

    barrier = pltpu.get_barrier_semaphore()
    for target in ((dp, right), (dp, left), (xn, mp), (yn, mp), (sib, mp)):
        pl.semaphore_signal(barrier, inc=1, device_id=target, device_id_type=MESH)
    pl.semaphore_wait(barrier, 5)

    half = rows // 2

    def slot(part, step, owner, piece):
        source = lax.rem(mp - step + n_mp, n_mp)
        first = owner * rows + (half if piece == 1 else 0)
        count = rows if piece is None else half
        return full_ref.at[part, source, pl.ds(pl.multiple_of(first, half), count), :]

    def copy(kind, part, step, owner, piece, target):
        index = (part * n_mp + step) * KINDS + kind
        place = slot(part, step, owner, piece)
        src = own_ref.at[part] if step == 0 and owner is dp else place
        return pltpu.make_async_remote_copy(
            src_ref=src, dst_ref=place, send_sem=send_sem.at[index], recv_sem=recv_sem.at[index],
            device_id=target, device_id_type=MESH,
        )

    def arrival(kind, part, step, sem_step, owner, piece):
        index = (part * n_mp + sem_step) * KINDS + kind
        place = slot(part, step, owner, piece)
        pltpu.make_async_remote_copy(
            src_ref=place, dst_ref=place, send_sem=send_sem.at[index], recv_sem=recv_sem.at[index],
            device_id=(sib, mp), device_id_type=MESH,
        ).wait_recv()

    sent = []

    def send(*args):
        item = copy(*args)
        item.start()
        sent.append(item)

    steps = [(part, step) for part in range(parts) for step in range(n_mp)]
    local = []
    for part in range(parts):
        item = pltpu.make_async_copy(own_ref.at[part], slot(part, 0, dp, None), local_sem.at[part])
        item.start()
        local.append(item)

    def along_ring(at):
        if at < len(steps):
            part, step = steps[at]
            if step > 0:
                arrival(Z, part, step, step - 1, dp, None)
            if step < n_mp - 1:
                send(Z, part, step, dp, None, (dp, right))

    along_ring(0)
    for at in range(len(steps) + 2):
        along_ring(at + 1)
        if at < len(steps):
            part, step = steps[at]
            send(X, part, step, dp, None, (xn, mp))
            send(Y, part, step, dp, None, (yn, mp))
            send(S_COL, part, step, dp, None, (sib, mp))
        if 0 <= at - 1 < len(steps):
            part, step = steps[at - 1]
            arrival(X, part, step, step, xn, None)
            send(D0, part, step, xn, 0, (yn, mp))
            send(S_X, part, step, xn, None, (sib, mp))
            arrival(Y, part, step, step, yn, None)
            send(D1, part, step, yn, 1, (xn, mp))
            send(S_Y, part, step, yn, None, (sib, mp))
        if 0 <= at - 2 < len(steps):
            part, step = steps[at - 2]
            arrival(D0, part, step, step, dn, 0)
            send(S_D0, part, step, dn, 0, (sib, mp))
            arrival(D1, part, step, step, dn, 1)
            send(S_D1, part, step, dn, 1, (sib, mp))
    for part, step in steps:
        arrival(S_COL, part, step, step, flip(dp, 1), None)
        arrival(S_X, part, step, step, flip(xn, 1), None)
        arrival(S_Y, part, step, step, flip(yn, 1), None)
        arrival(S_D0, part, step, step, flip(dn, 1), 0)
        arrival(S_D1, part, step, step, flip(dn, 1), 1)
    for item in sent:
        item.wait_send()
    for item in local:
        item.wait()


def gather_weights(own, n_dp, n_mp):
    parts, rows, columns = own.shape
    if n_dp != 2 ** 3:
        full = lax.all_gather(own, "dp", axis=1, tiled=True)
        return lax.all_gather(full, "mp", axis=1)
    count = parts * n_mp * KINDS
    return pl.pallas_call(
        functools.partial(gather_kernel, n_mp),
        out_shape=jax.ShapeDtypeStruct((parts, n_mp, n_dp * rows, columns), own.dtype),
        in_specs=[pl.BlockSpec(memory_space=pltpu.VMEM)],
        out_specs=pl.BlockSpec(memory_space=pl.ANY),
        scratch_shapes=[
            pltpu.SemaphoreType.DMA((count,)),
            pltpu.SemaphoreType.DMA((count,)),
            pltpu.SemaphoreType.DMA((parts,)),
        ],
        compiler_params=pltpu.CompilerParams(collective_id=0, has_side_effects=True),
        name="gather_weights",
    )(own)


def layer_norm(values, gain):
    centre = values - jnp.mean(values, axis=-1, keepdims=True)
    spread = jnp.mean(centre * centre, axis=-1, keepdims=True)
    return centre * lax.rsqrt(spread + 1e-06) * gain


def unit_rows(values):
    return values * lax.rsqrt(jnp.sum(values * values, axis=-1, keepdims=True) + 1e-06)


def dot(left, right):
    return jnp.dot(left, right, preferred_element_type=jnp.float32)


def dot_t(left, right):
    return lax.dot_general(left, right, (((1,), (1,)), ((), ())), preferred_element_type=jnp.float32)


def grouped(values):
    return values.astype(jnp.bfloat16).astype(jnp.float32)


def shards(
    patches,
    gain_first,
    joint_weight,
    head_scale,
    output_weight,
    gain_second,
    up_weight,
    down_weight,
    gain_final,
    project_weight,
    text_bank,
    captions,
    reference_loss,
):
    n_dp, n_mp = lax.axis_size("dp"), lax.axis_size("mp")
    own_images, patch_count, features = patches.shape
    rows = joint_weight.shape[0]
    local_heads = head_scale.shape[0]
    width = joint_weight.shape[2]
    head_width = width // local_heads
    tokens = own_images * patch_count

    attention_part = jnp.concatenate([joint_weight.reshape(rows, 3 * width), output_weight.T], axis=1)
    own = jnp.stack([attention_part, up_weight, down_weight.T])
    full = gather_weights(own, n_dp, n_mp)
    scales = lax.all_gather(head_scale, "mp", axis=0, tiled=True)

    residual = patches.astype(jnp.float32).reshape(tokens, features)
    normed_first = layer_norm(residual, gain_first).astype(jnp.bfloat16)
    joint = jnp.stack([dot(normed_first, full[0, m, :, : 3 * width]) for m in range(n_mp)], axis=1)
    joint = joint.reshape(own_images, patch_count, n_mp, 3, local_heads, head_width)
    queries = unit_rows(joint[:, :, :, 0]).astype(jnp.bfloat16)
    key_rows = unit_rows(joint[:, :, :, 1]).astype(jnp.bfloat16)
    value_rows = joint[:, :, :, 2].astype(jnp.bfloat16)
    scores = jnp.einsum("bqmhd,bkmhd->bmhqk", queries, key_rows, preferred_element_type=jnp.float32)
    exponent = jnp.exp(scores * scales.reshape(n_mp, local_heads)[None, :, :, None, None])
    attention = (exponent / jnp.sum(exponent, axis=-1, keepdims=True)).astype(jnp.bfloat16)
    head_out = jnp.einsum(
        "bmhqk,bkmhd->bqmhd", attention, value_rows, preferred_element_type=jnp.float32
    ).astype(jnp.bfloat16).reshape(tokens, n_mp, width)
    residual_two = residual
    for m in range(n_mp):
        residual_two = residual_two + grouped(dot_t(head_out[:, m], full[0, m, :, 3 * width :]))
    normed_second = layer_norm(residual_two, gain_second).astype(jnp.bfloat16)
    total = residual_two
    for m in range(n_mp):
        hidden = jax.nn.gelu(dot(normed_second, full[1, m]), approximate=False).astype(jnp.bfloat16)
        total = total + grouped(dot_t(hidden, full[2, m]))
    pooled = jnp.sum(total.reshape(own_images, patch_count, features), axis=1) / patch_count
    pooled_norm = layer_norm(pooled, gain_final).astype(jnp.bfloat16)
    image_units = unit_rows(dot(pooled_norm, project_weight)).astype(jnp.bfloat16)

    place = lax.axis_index(("dp", "mp"))
    texts = text_bank.shape[0]
    all_units = lax.all_gather(image_units, ("dp", "mp"), axis=0, tiled=True)
    logits = dot_t(all_units, text_bank)
    highest = jnp.max(logits, axis=1)
    totals = jnp.sum(jnp.exp(logits - highest[:, None]), axis=1)
    text_ids = lax.broadcasted_iota(jnp.int32, logits.shape, 1) + place * texts
    matched = jnp.sum(jnp.where(text_ids == captions[:, None], logits, 0.0), axis=1)
    stats = jnp.stack([highest, totals, matched])
    everyone = lax.all_gather(stats, ("dp", "mp"), axis=0)
    mine = lax.dynamic_slice_in_dim(everyone, place * own_images, own_images, axis=2)
    top = jnp.max(mine[:, 0], axis=0)
    total_exp = jnp.sum(mine[:, 1] * jnp.exp(mine[:, 0] - top[None]), axis=0)
    return top + jnp.log(total_exp) - jnp.sum(mine[:, 2], axis=0) - reference_loss


def solution(mesh):
    placed = (
        P(("dp", "mp"), None, None),
        P(),
        P("dp", None, "mp"),
        P("mp"),
        P("mp", "dp"),
        P(),
        P("dp", "mp"),
        P("mp", "dp"),
        P(),
        P(),
        P(("dp", "mp"), None),
        P(),
        P(("dp", "mp")),
    )
    return jax.shard_map(
        shards, mesh=mesh, in_specs=placed, out_specs=P(("dp", "mp")), check_vma=False
    )
```

time: 442 us -> 381 us (0.86)
  waiting for transfers between devices: 359 us -> 0 us
  blocking collectives: 12.7 us -> 153 us
  Pallas kernels: 0 us -> 122 us
  local copies, waits for them, and re-layouts: 2.06 us -> 28.7 us
  matrix products: 38.9 us -> 61.9 us
  between operations: 15.1 us -> 1.38 us
    all_gather x6 -> x0, waiting for transfers between devices: 239 us -> none  [the longest x2 130 us: gather_images(): return lax.all_gather(values, 'mp', axis=0, tiled=True)]
    pallas_call x0 -> x1, Pallas kernels: none -> 122 us  [gather_weights(): pl.pallas_call(functools.partial(gather_kernel, n_mp), out_shape=jax.Shap...]
    all_gather x1 -> x2, blocking collectives: 12.7 us -> 133 us  [the longest x1 67.1 us: shards(): all_units = lax.all_gather(image_units, ('dp', 'mp'), axis=0, tiled=True)]
    reduce_scatter x2 -> x0, waiting for transfers between devices: 119 us -> none  [group_sums(): lax.psum_scatter(term.astype(jnp.bfloat16), 'mp', scatter_dimension=0, ti...]
    dot_general x7 -> x16, matrix products: 38.9 us -> 61.9 us  [the longest x9 40.1 us: dot_t(): lax.dot_general(left, right, (((1,), (1,)), ((), ())), preferred_element_...]
    unnamed x0 -> x1, blocking collectives: none -> 20.2 us
    dot_general x0 -> x5, local copies, waits for them, and re-layouts: none -> 15.9 us  [dot(): return jnp.dot(left, right, preferred_element_type=jnp.float32)]
  transfers between devices with their start and end apart: 8 -> 0, of which waited for: 8 -> 0; matrix products, arithmetic and copies ran while one was open for 3% -> 0% of each run, Pallas kernels for 0% -> 0%
where the time goes in v1:
time: 381 us; the launch traced here: 378 us
  blocking collectives  153 us (40%)
  Pallas kernels  122 us (32%)
  matrix products  61.9 us (16%)
  local copies, waits for them, and re-layouts  28.7 us (8%)
  other arithmetic  10.6 us (3%)
    pallas_call x1, Pallas kernels, gather_weights(): pl.pallas_call(functools.partial(gather_kernel, n_mp), out_shape=jax.Shap...  122 us
    all_gather x1, blocking collectives, shards(): all_units = lax.all_gather(image_units, ('dp', 'mp'), axis=0, tiled=True)  67.1 us
    all_gather x1, blocking collectives, shards(): everyone = lax.all_gather(stats, ('dp', 'mp'), axis=0)  65.9 us
    dot_general x9, matrix products, dot_t(): lax.dot_general(left, right, (((1,), (1,)), ((), ())), preferred_element_...  40.1 us
    unnamed x1, blocking collectives  20.2 us
    dot_general x5, local copies, waits for them, and re-layouts, dot(): return jnp.dot(left, right, preferred_element_type=jnp.float32)  15.9 us
    dot_general x5, matrix products, dot(): return jnp.dot(left, right, preferred_element_type=jnp.float32)  15.1 us

profile of v1, /device:TPU:0, one launch (start us, length us, event | category | flops | bytes accessed | tf_op | source)
XLA Modules:
  0.0 377.6 jit_solution(3295106984572476856)
XLA Ops:
  0.0 1.2 copy.54
  1.2 0.2 copy.56
  1.4 0.9 copy.55
  2.4 0.1 copy.57
  2.5 1.0 pad_maximum_fusion.1.own_ref
  3.6 121.8 %gather_weights.1 = bf16[3,4,1024,1024]{3,2,1,0:T(8,128)(2,1)} custom-call(bf16[3,128,1024]{2,1,0:T(8,128)(2,1)} %pad_maximum_fusion.1.own_ref), custom_call_target="tpu_custom_call" | custom-call | tf_op jit(solution)/shard_map/gather_weights/pallas_call | solution.py:118
  125.4 5.5 %slice_bitcast_fusion.5 = (bf16[768,1024]{0,1:T(8,128)(2,1)}, bf16[768,1024]{0,1:T(8,128)(2,1)}, bf16[768,1024]{0,1:T(8,128)(2,1)}, bf16[768,1024]{0,1:T(8,128)(2,1)}) fusion(bf16[3,4,1024,1024]{3,2,1,0:T(8,128)(2,1)} %gather_weights.1), kind=kLoop, calls=%fused_computation.124 | loop fusion | bytes 12582912 | tf_op jit(solution)/shard_map/dot_general | solution.py:144
  130.9 2.7 copy.60
  133.6 0.2 convert_reduce_fusion
  133.8 0.3 multiply_reduce_fusion.3
  134.1 0.9 copy-done.8
  135.0 3.0 convolution_bitcast_fusion.1
  137.9 2.6 copy.59
  140.5 4.3 %convolution_bitcast_fusion.2 = f32[6,64,1,3,4,64]{1,5,4,3,0,2:T(8,128)} fusion(bf16[3,4,64,1024,1]{3,2,1,0,4:T(8,128)(2,1)} %bitcast.181, bf16[6,64,1024]{2,1,0:T(8,128)(2,1)S(1)} %copy-done.2, f32[1024]{0:T(1024)S(1)} %copy-done.15, f32[6,64]{1,0:T(8,128)S(1)} %add_rsqrt_fusion.2, f32[6,64]{1,0:T(8,128)S(1)} %broadcast_multiply_fusion), kind=kOutput, calls=%fused_computation.41 | convolution fusion | flops 605945856 | bytes 3546112 | tf_op jit(solution)/shard_map/dot_general | solution.py:144
  144.9 2.6 copy.58
  147.5 4.3 %convolution_bitcast_fusion.3 = f32[6,64,1,3,4,64]{1,5,4,3,0,2:T(8,128)} fusion(bf16[3,4,64,1024,1]{3,2,1,0,4:T(8,128)(2,1)} %bitcast.182, bf16[6,64,1024]{2,1,0:T(8,128)(2,1)S(1)} %copy-done.2, f32[1024]{0:T(1024)S(1)} %copy-done.15, f32[6,64]{1,0:T(8,128)S(1)} %add_rsqrt_fusion.2, f32[6,64]{1,0:T(8,128)S(1)} %broadcast_multiply_fusion), kind=kOutput, calls=%fused_computation.42 | convolution fusion | flops 605945856 | bytes 3546112 | tf_op jit(solution)/shard_map/dot_general | solution.py:144
  151.7 2.6 copy.61
  154.3 3.0 convolution_bitcast_fusion
  157.4 0.5 copy-done.7
  157.9 1.3 pad_maximum_fusion
  159.2 1.2 multiply_reduce_fusion.1
  160.5 3.3 multiply_convert_fusion.1
  163.8 0.6 dynamic-slice
  165.0 0.2 dynamic-update-slice
  165.3 20.2 %all-reduce = f32[16]{0:T(128)S(1)} all-reduce(f32[16]{0:T(128)S(1)} %dynamic-update-slice), channel_id=1, replica_groups=mesh['dp'=8,'mp'=4] {'mp'}, use_global_device_ids=true, to_apply=%add | all-reduce | flops 16 | bytes 128
  185.6 2.9 fusion
  188.5 3.8 %fusion.74 = bf16[6,64,4,4,64]{1,4,3,2,0:T(8,128)(2,1)} fusion(f32[6,4,4,64,64]{3,4,2,1,0:T(8,128)S(1)} %get-tuple-element.19, f32[6,4,4,64]{3,2,1,0:T(4,128)S(1)} %get-tuple-element.18, f32[4,4]{1,0:T(4,128)S(1)} %mul.168, f32[6,64,4,3,4,64]{1,5,4,3,0,2:T(8,128)} %copy-done.1), kind=kOutput, calls=%fused_computation.135 | convolution fusion | flops 51904512 | bytes 3956800 | tf_op jit(solution)/shard_map/bmhqk,bkmhd->bqmhd/dot_general | solution.py:193
  192.3 3.8 copy.66
  196.1 2.8 reshape.194
  198.9 1.4 convolution_convert_fusion.4
  200.4 1.4 convolution_convert_fusion.3
  201.8 1.4 convolution_convert_fusion.2
  203.3 1.7 fusion.367
  205.0 1.2 copy-done.3
  206.2 0.3 multiply_reduce_fusion.2
  206.6 8.6 %fusion.77 = bf16[384,1024]{1,0:T(8,128)(2,1)} fusion(bf16[3,4,1024,1024]{3,2,1,0:T(8,128)(2,1)} %gather_weights.1, f32[384,1024]{1,0:T(8,128)} %copy-done.3, f32[1024]{0:T(1024)S(1)} %copy-done.16, f32[384]{0:T(512)S(1)} %add_rsqrt_fusion.3, f32[384]{0:T(512)S(1)} %broadcast_multiply_fusion.1), kind=kOutput, calls=%fused_computation.141 | convolution fusion | flops 1638137856 | bytes 6560768 | tf_op jit(solution)/shard_map/dot_general | solution.py:148
  215.1 8.0 %fusion.80 = bf16[384,1024]{1,0:T(8,128)(2,1)} fusion(bf16[3,4,1024,1024]{3,2,1,0:T(8,128)(2,1)} %gather_weights.1, f32[384,1024]{1,0:T(8,128)S(1)} %copy-done.4, f32[1024]{0:T(1024)S(1)} %copy-done.16, f32[384]{0:T(512)S(1)} %add_rsqrt_fusion.3, f32[384]{0:T(512)S(1)} %broadcast_multiply_fusion.1), kind=kOutput, calls=%fused_computation.142 | convolution fusion | flops 1638137856 | bytes 6560768 | tf_op jit(solution)/shard_map/dot_general | solution.py:148
  223.1 8.2 %fusion.83 = bf16[384,1024]{1,0:T(8,128)(2,1)} fusion(bf16[3,4,1024,1024]{3,2,1,0:T(8,128)(2,1)} %gather_weights.1, f32[384,1024]{1,0:T(8,128)S(1)} %copy-done.4, f32[1024]{0:T(1024)S(1)} %copy-done.16, f32[384]{0:T(512)S(1)} %add_rsqrt_fusion.3, f32[384]{0:T(512)S(1)} %broadcast_multiply_fusion.1), kind=kOutput, calls=%fused_computation.143 | convolution fusion | flops 1638137856 | bytes 6560768 | tf_op jit(solution)/shard_map/dot_general | solution.py:148
  231.3 9.0 %convert_add_fusion = f32[384,1024]{1,0:T(8,128)} fusion(bf16[384,1024]{1,0:T(8,128)(2,1)} %fusion.83, bf16[384,1024]{1,0:T(8,128)(2,1)} %fusion.80, f32[384,1024]{1,0:T(8,128)S(1)} %copy-done.4, bf16[384,1024]{1,0:T(8,128)(2,1)} %fusion.77, bf16[3,4,1024,1024]{3,2,1,0:T(8,128)(2,1)} %gather_weights.1, f32[1024]{0:T(1024)S(1)} %copy-done.16, ...), kind=kOutput, calls=%fused_computation.65 | convolution fusion | flops 1641283584 | bytes 11280384 | tf_op jit(solution)/shard_map/dot_general | solution.py:148
  240.3 1.6 reduce_sum.142
  241.9 0.1 multiply_reduce_fusion.5
  242.1 0.2 multiply_reduce_fusion.4
  242.3 0.5 multiply_reduce_fusion.6
  242.9 67.1 %all-gather.1 = bf16[32,6,768]{2,1,0:T(8,128)(2,1)S(1)} all-gather(bf16[1,6,768]{2,1,0:T(8,128)(2,1)S(1)} %fusion.241), channel_id=1, replica_groups=mesh['dp'=8,'mp'=4] {'dp','mp'}, dimensions={0}, use_global_device_ids=true | all-gather | bytes 304128 | tf_op jit(solution)/shard_map/all_gather | solution.py:210
  310.1 0.3 fusion.368
  310.5 65.9 %all-gather.2 = f32[32,3,192]{2,1,0:T(4,128)S(1)} all-gather(f32[1,3,192]{2,1,0:T(4,128)S(1)} %maximum_bitcast_fusion.1), channel_id=2, replica_groups=mesh['dp'=8,'mp'=4] {'dp','mp'}, dimensions={0}, use_global_device_ids=true | all-gather | bytes 76032 | tf_op jit(solution)/shard_map/all_gather | solution.py:217
  376.4 0.2 constant_dynamic-slice_fusion
  376.6 0.5 subtract_subtract_fusion
  (53 shorter events, 0.6 us)
Async XLA Ops:
  0.0 242.3 %copy-start = (bf16[1024,768]{1,0:T(8,128)(2,1)S(1)}, bf16[1024,768]{1,0:T(8,128)(2,1)}, u32[]{:S(2)}) copy-start(bf16[1024,768]{1,0:T(8,128)(2,1)} %param.22) | copy-start | bytes 4718596
  0.0 2.4 copy-start.9
  0.0 2.5 copy-start.10
  130.9 2.7 copy-start.2
  133.6 1.4 copy-start.8
  133.6 1.4 copy-start.15
  154.3 3.1 copy-start.5
  154.3 3.1 copy-start.6
  154.3 3.6 copy-start.7
  159.2 4.6 %copy-start.1 = (f32[6,64,4,3,4,64]{1,5,4,3,0,2:T(8,128)}, f32[6,64,4,3,4,64]{1,5,4,3,0,2:T(8,128)S(1)}, u32[]{:S(2)}) copy-start(f32[6,64,4,3,4,64]{1,5,4,3,0,2:T(8,128)S(1)} %pad_maximum_fusion) | copy-start | bytes 14155780
  160.5 3.3 copy-start.18
  160.5 4.5 %copy-start.17 = (f32[4]{0:T(128)S(1)}, f32[4]{0:T(128)}, u32[]{:S(2)}) copy-start(f32[4]{0:T(128)} %param.16) | copy-start | bytes 52
  205.0 1.2 copy-start.3
  205.0 1.5 copy-start.16
  206.6 8.6 %copy-start.4 = (f32[384,1024]{1,0:T(8,128)S(1)}, f32[384,1024]{1,0:T(8,128)}, u32[]{:S(2)}) copy-start(f32[384,1024]{1,0:T(8,128)} %copy-done.3) | copy-start | bytes 4718596
  240.3 1.9 copy-start.12
  241.9 68.1 %copy-start.11 = (bf16[96,768]{1,0:T(8,128)(2,1)S(1)}, bf16[96,768]{1,0:T(8,128)(2,1)}, u32[]{:S(2)}) copy-start(bf16[96,768]{1,0:T(8,128)(2,1)} %param.23) | copy-start | bytes 442372
  242.3 68.1 %copy-start.13 = (s32[192]{0:T(256)S(1)}, s32[192]{0:T(256)}, u32[]{:S(2)}) copy-start(s32[192]{0:T(256)} %param.24) | copy-start | bytes 2308
  242.3 134.4 %copy-start.14 = (f32[6]{0:T(128)S(1)}, f32[6]{0:T(128)}, u32[]{:S(2)}) copy-start(f32[6]{0:T(128)} %param.25) | copy-start | bytes 76

commit v2 on v1

--- a/solution.py
+++ b/solution.py
@@ -16,7 +16,9 @@
     return index + bit - 2 * bit * ((index // bit) % 2)
 
 
-def gather_kernel(n_mp, own_ref, full_ref, send_sem, recv_sem, local_sem):
+def gather_kernel(
+    n_mp, own_ref, scale_ref, full_ref, scales_ref, send_sem, recv_sem, local_sem, scale_send, scale_recv
+):
     parts, rows, _ = own_ref.shape
     dp, mp = lax.axis_index("dp"), lax.axis_index("mp")
     sib, xn, yn = flip(dp, 1), flip(dp, 2), flip(dp, 4)
@@ -53,6 +55,21 @@
             device_id=(sib, mp), device_id_type=MESH,
         ).wait_recv()
 
+    def scale_copy(step, source):
+        return pltpu.make_async_remote_copy(
+            src_ref=scale_ref if step == 0 else scales_ref.at[source], dst_ref=scales_ref.at[source],
+            send_sem=scale_send.at[step], recv_sem=scale_recv.at[step],
+            device_id=(dp, right), device_id_type=MESH,
+        )
+
+    def scale_step(step):
+        if step > 0:
+            scale_copy(step - 1, lax.rem(mp - step + n_mp, n_mp)).wait_recv()
+        if step < n_mp - 1:
+            item = scale_copy(step, lax.rem(mp - step + n_mp, n_mp))
+            item.start()
+            sent.append(item)
+
     sent = []
 
     def send(*args):
@@ -66,10 +83,15 @@
         item = pltpu.make_async_copy(own_ref.at[part], slot(part, 0, dp, None), local_sem.at[part])
         item.start()
         local.append(item)
+    item = pltpu.make_async_copy(scale_ref, scales_ref.at[mp], local_sem.at[parts])
+    item.start()
+    local.append(item)
 
     def along_ring(at):
         if at < len(steps):
             part, step = steps[at]
+            if part == 0:
+                scale_step(step)
             if step > 0:
                 arrival(Z, part, step, step - 1, dp, None)
             if step < n_mp - 1:
@@ -109,25 +131,119 @@
         item.wait()
 
 
-def gather_weights(own, n_dp, n_mp):
+def gather_weights(own, scale, n_dp, n_mp):
     parts, rows, columns = own.shape
     if n_dp != 2 ** 3:
         full = lax.all_gather(own, "dp", axis=1, tiled=True)
-        return lax.all_gather(full, "mp", axis=1)
+        return lax.all_gather(full, "mp", axis=1), lax.all_gather(scale, "mp", axis=0)
     count = parts * n_mp * KINDS
     return pl.pallas_call(
         functools.partial(gather_kernel, n_mp),
-        out_shape=jax.ShapeDtypeStruct((parts, n_mp, n_dp * rows, columns), own.dtype),
-        in_specs=[pl.BlockSpec(memory_space=pltpu.VMEM)],
-        out_specs=pl.BlockSpec(memory_space=pl.ANY),
+        out_shape=(
+            jax.ShapeDtypeStruct((parts, n_mp, n_dp * rows, columns), own.dtype),
+            jax.ShapeDtypeStruct((n_mp, *scale.shape), scale.dtype),
+        ),
+        in_specs=[pl.BlockSpec(memory_space=pltpu.VMEM)] * 2,
+        out_specs=(pl.BlockSpec(memory_space=pl.ANY), pl.BlockSpec(memory_space=pltpu.VMEM)),
         scratch_shapes=[
             pltpu.SemaphoreType.DMA((count,)),
             pltpu.SemaphoreType.DMA((count,)),
-            pltpu.SemaphoreType.DMA((parts,)),
+            pltpu.SemaphoreType.DMA((parts + 1,)),
+            pltpu.SemaphoreType.DMA((n_mp,)),
+            pltpu.SemaphoreType.DMA((n_mp,)),
         ],
         compiler_params=pltpu.CompilerParams(collective_id=0, has_side_effects=True),
         name="gather_weights",
+    )(own, scale)
+
+
+def exchange_kernel(n_dp, n_mp, spread, own_ref, all_ref, send_sem, recv_sem, local_sem):
+    dp, mp = lax.axis_index("dp"), lax.axis_index("mp")
+    count = n_dp * n_mp
+    me = dp * n_mp + mp
+    barrier = pltpu.get_barrier_semaphore()
+
+    def peer(shift):
+        other = lax.rem(me + shift, count)
+        return other, (other // n_mp, lax.rem(other, n_mp))
+
+    def greet(shift, carry):
+        pl.semaphore_signal(barrier, inc=1, device_id=peer(shift)[1], device_id_type=MESH)
+        return carry
+
+    lax.fori_loop(1, count, greet, 0)
+    pl.semaphore_wait(barrier, count - 1)
+    local = pltpu.make_async_copy(own_ref.at[me] if spread else own_ref, all_ref.at[me], local_sem)
+    local.start()
+
+    def copy(shift):
+        other, target = peer(shift)
+        return pltpu.make_async_remote_copy(
+            src_ref=own_ref.at[other] if spread else own_ref, dst_ref=all_ref.at[me],
+            send_sem=send_sem.at[shift], recv_sem=recv_sem.at[shift],
+            device_id=target, device_id_type=MESH,
+        )
+
+    def begin(shift, carry):
+        copy(shift).start()
+        return carry
+
+    def finish(shift, carry):
+        source = lax.rem(me - shift + count, count)
+        pltpu.make_async_remote_copy(
+            src_ref=all_ref.at[source], dst_ref=all_ref.at[source],
+            send_sem=send_sem.at[shift], recv_sem=recv_sem.at[shift],
+            device_id=peer(shift)[1], device_id_type=MESH,
+        ).wait_recv()
+        copy(shift).wait_send()
+        return carry
+
+    lax.fori_loop(1, count, begin, 0)
+    lax.fori_loop(1, count, finish, 0)
+    local.wait()
+
+
+def exchange(own, n_dp, n_mp, spread, collective_id):
+    count = n_dp * n_mp
+    block = own.shape[1:] if spread else own.shape
+    return pl.pallas_call(
+        functools.partial(exchange_kernel, n_dp, n_mp, spread),
+        out_shape=jax.ShapeDtypeStruct((count, *block), own.dtype),
+        in_specs=[pl.BlockSpec(memory_space=pltpu.VMEM)],
+        out_specs=pl.BlockSpec(memory_space=pltpu.VMEM),
+        scratch_shapes=[
+            pltpu.SemaphoreType.DMA((count,)),
+            pltpu.SemaphoreType.DMA((count,)),
+            pltpu.SemaphoreType.DMA,
+        ],
+        compiler_params=pltpu.CompilerParams(collective_id=collective_id, has_side_effects=True),
+        name="spread_stats" if spread else "share_units",
     )(own)
+
+
+def feed_kernel(normed_ref, up_ref, down_ref, residual_ref, total_ref):
+    @pl.when(pl.program_id(0) == 0)
+    def _():
+        total_ref[...] = residual_ref[...]
+
+    upper = dot(normed_ref[...], up_ref[...])
+    hidden = (0.5 * upper * (1.0 + lax.erf(upper * 0.5 ** 0.5))).astype(jnp.bfloat16)
+    total_ref[...] += grouped(dot_t(hidden, down_ref[...]))
+
+
+def feed_forward(normed, full, residual):
+    _, groups, features, width = full.shape
+    weight = lambda part: pl.BlockSpec((None, None, features, width), lambda m: (part, m, 0, 0))
+    whole = pl.BlockSpec(normed.shape, lambda m: (0, 0))
+    return pl.pallas_call(
+        feed_kernel,
+        grid=(groups,),
+        out_shape=jax.ShapeDtypeStruct(residual.shape, jnp.float32),
+        in_specs=[whole, weight(1), weight(2), whole],
+        out_specs=whole,
+        compiler_params=pltpu.CompilerParams(dimension_semantics=("arbitrary",)),
+        name="feed_forward",
+    )(normed, full, full, residual)
 
 
 def layer_norm(values, gain):
@@ -177,45 +293,40 @@
 
     attention_part = jnp.concatenate([joint_weight.reshape(rows, 3 * width), output_weight.T], axis=1)
     own = jnp.stack([attention_part, up_weight, down_weight.T])
-    full = gather_weights(own, n_dp, n_mp)
-    scales = lax.all_gather(head_scale, "mp", axis=0, tiled=True)
+    full, scales = gather_weights(own, head_scale[None, :], n_dp, n_mp)
 
     residual = patches.astype(jnp.float32).reshape(tokens, features)
     normed_first = layer_norm(residual, gain_first).astype(jnp.bfloat16)
-    joint = jnp.stack([dot(normed_first, full[0, m, :, : 3 * width]) for m in range(n_mp)], axis=1)
-    joint = joint.reshape(own_images, patch_count, n_mp, 3, local_heads, head_width)
-    queries = unit_rows(joint[:, :, :, 0]).astype(jnp.bfloat16)
-    key_rows = unit_rows(joint[:, :, :, 1]).astype(jnp.bfloat16)
-    value_rows = joint[:, :, :, 2].astype(jnp.bfloat16)
-    scores = jnp.einsum("bqmhd,bkmhd->bmhqk", queries, key_rows, preferred_element_type=jnp.float32)
-    exponent = jnp.exp(scores * scales.reshape(n_mp, local_heads)[None, :, :, None, None])
-    attention = (exponent / jnp.sum(exponent, axis=-1, keepdims=True)).astype(jnp.bfloat16)
-    head_out = jnp.einsum(
-        "bmhqk,bkmhd->bqmhd", attention, value_rows, preferred_element_type=jnp.float32
-    ).astype(jnp.bfloat16).reshape(tokens, n_mp, width)
     residual_two = residual
     for m in range(n_mp):
-        residual_two = residual_two + grouped(dot_t(head_out[:, m], full[0, m, :, 3 * width :]))
+        joint = dot(normed_first, full[0, m])[:, : 3 * width]
+        joint = joint.reshape(own_images, patch_count, 3, local_heads, head_width)
+        queries = unit_rows(joint[:, :, 0]).astype(jnp.bfloat16)
+        key_rows = unit_rows(joint[:, :, 1]).astype(jnp.bfloat16)
+        value_rows = joint[:, :, 2].astype(jnp.bfloat16)
+        scores = jnp.einsum("bqhd,bkhd->bhqk", queries, key_rows, preferred_element_type=jnp.float32)
+        exponent = jnp.exp(scores * scales[m, 0][None, :, None, None])
+        attention = (exponent / jnp.sum(exponent, axis=-1, keepdims=True)).astype(jnp.bfloat16)
+        head_out = jnp.einsum(
+            "bhqk,bkhd->bqhd", attention, value_rows, preferred_element_type=jnp.float32
+        ).astype(jnp.bfloat16).reshape(tokens, width)
+        residual_two = residual_two + grouped(dot_t(head_out, full[0, m, :, 3 * width :]))
     normed_second = layer_norm(residual_two, gain_second).astype(jnp.bfloat16)
-    total = residual_two
-    for m in range(n_mp):
-        hidden = jax.nn.gelu(dot(normed_second, full[1, m]), approximate=False).astype(jnp.bfloat16)
-        total = total + grouped(dot_t(hidden, full[2, m]))
+    total = feed_forward(normed_second, full, residual_two)
     pooled = jnp.sum(total.reshape(own_images, patch_count, features), axis=1) / patch_count
     pooled_norm = layer_norm(pooled, gain_final).astype(jnp.bfloat16)
     image_units = unit_rows(dot(pooled_norm, project_weight)).astype(jnp.bfloat16)
 
     place = lax.axis_index(("dp", "mp"))
     texts = text_bank.shape[0]
-    all_units = lax.all_gather(image_units, ("dp", "mp"), axis=0, tiled=True)
+    all_units = exchange(image_units, n_dp, n_mp, False, 1).reshape(-1, image_units.shape[1])
     logits = dot_t(all_units, text_bank)
     highest = jnp.max(logits, axis=1)
     totals = jnp.sum(jnp.exp(logits - highest[:, None]), axis=1)
     text_ids = lax.broadcasted_iota(jnp.int32, logits.shape, 1) + place * texts
     matched = jnp.sum(jnp.where(text_ids == captions[:, None], logits, 0.0), axis=1)
-    stats = jnp.stack([highest, totals, matched])
-    everyone = lax.all_gather(stats, ("dp", "mp"), axis=0)
-    mine = lax.dynamic_slice_in_dim(everyone, place * own_images, own_images, axis=2)
+    stats = jnp.stack([highest, totals, matched]).reshape(3, n_dp * n_mp, own_images)
+    mine = exchange(stats.transpose(1, 0, 2), n_dp, n_mp, True, 2)
     top = jnp.max(mine[:, 0], axis=0)
     total_exp = jnp.sum(mine[:, 1] * jnp.exp(mine[:, 0] - top[None]), axis=0)
     return top + jnp.log(total_exp) - jnp.sum(mine[:, 2], axis=0) - reference_loss

time: 381 us -> 242 us (0.64)
  blocking collectives: 153 us -> 0 us
  Pallas kernels: 122 us -> 159 us
  matrix products: 61.9 us -> 30.4 us
  local copies, waits for them, and re-layouts: 28.7 us -> 37.4 us
    all_gather x2 -> x0, blocking collectives: 133 us -> none  [the longest x1 67.1 us: shards(): all_units = lax.all_gather(image_units, ('dp', 'mp'), axis=0, tiled=True)]
    pallas_call x1 -> x4, Pallas kernels: 122 us -> 159 us  [the longest x1 123 us: gather_weights(): pl.pallas_call(functools.partial(gather_kernel, n_mp), out_shape=(jax.Sha...]
    dot_general x9 -> x5, matrix products: 40.1 us -> 8.81 us  [dot_t(): lax.dot_general(left, right, (((1,), (1,)), ((), ())), preferred_element_...]
    unnamed x1 -> x0, blocking collectives: 20.2 us -> none
    dot_general x5 -> x0, local copies, waits for them, and re-layouts: 15.9 us -> none  [dot(): return jnp.dot(left, right, preferred_element_type=jnp.float32)]
    slice x0 -> x8, local copies, waits for them, and re-layouts: none -> 11 us  [the longest x4 5.9 us: shards(): key_rows = unit_rows(joint[:, :, 1]).astype(jnp.bfloat16)]
    reshape x1 -> x9, local copies, waits for them, and re-layouts: 2.84 us -> 12.8 us  [the longest x4 9.88 us: shards(): joint = joint.reshape(own_images, patch_count, 3, local_heads, head_width)]
    dot_general x5, matrix products: 15.1 us -> 7.58 us  [dot(): return jnp.dot(left, right, preferred_element_type=jnp.float32)]
where the time goes in v2:
time: 242 us; the launch traced here: 241 us
  Pallas kernels  159 us (66%)
  local copies, waits for them, and re-layouts  37.4 us (15%)
  matrix products  30.4 us (13%)
  other arithmetic  13.3 us (5%)
    pallas_call x1, Pallas kernels, gather_weights(): pl.pallas_call(functools.partial(gather_kernel, n_mp), out_shape=(jax.Sha...  123 us
    pallas_call x2, Pallas kernels, exchange(): pl.pallas_call(functools.partial(exchange_kernel, n_dp, n_mp, spread), ou...  24.7 us
    pallas_call x1, Pallas kernels, feed_forward(): pl.pallas_call(feed_kernel, grid=(groups,), out_shape=jax.ShapeDtypeStruc...  11.9 us
    reshape x4, local copies, waits for them, and re-layouts, shards(): joint = joint.reshape(own_images, patch_count, 3, local_heads, head_width)  9.88 us
    dot_general x5, matrix products, dot_t(): lax.dot_general(left, right, (((1,), (1,)), ((), ())), preferred_element_...  8.81 us
    dot_general x4, matrix products, shards(): jnp.einsum('bhqk,bkhd->bqhd', attention, value_rows, preferred_element_ty...  7.8 us
    dot_general x5, matrix products, dot(): return jnp.dot(left, right, preferred_element_type=jnp.float32)  7.58 us
    dot_general x4, matrix products, shards(): jnp.einsum('bqhd,bkhd->bhqk', queries, key_rows, preferred_element_type=j...  6.17 us

profile of v2, /device:TPU:0, one launch (start us, length us, event | category | flops | bytes accessed | tf_op | source)
XLA Modules:
  0.0 241.0 jit_solution(7212296146143258116)
XLA Ops:
  0.5 1.4 convert_reduce_fusion
  1.9 1.5 multiply_reduce_fusion.1
  4.1 1.0 pad_maximum_fusion.own_ref
  5.5 122.8 %gather_weights.1 = (bf16[3,4,1024,1024]{3,2,1,0:T(8,128)(2,1)}, f32[4,1,4]{2,1,0:T(1,128)}) custom-call(bf16[3,128,1024]{2,1,0:T(8,128)(2,1)} %pad_maximum_fusion.own_ref, f32[1,4]{1,0:T(1,128)} %bitcast.164), custom_call_target="tpu_custom_call" | custom-call | tf_op jit(solution)/shard_map/gather_weights/pallas_call | solution.py:140
  128.9 5.7 %slice_bitcast_fusion = (bf16[1024,1024]{1,0:T(8,128)(2,1)S(1)}, bf16[1024,1024]{1,0:T(8,128)(2,1)}, bf16[1024,1024]{1,0:T(8,128)(2,1)}, bf16[1024,1024]{1,0:T(8,128)(2,1)}) fusion(bf16[3,4,1024,1024]{3,2,1,0:T(8,128)(2,1)} %get-tuple-element.7.up_ref.down_ref), kind=kLoop, calls=%fused_computation | loop fusion | bytes 16777216 | tf_op jit(solution)/shard_map/squeeze | solution.py:302
  134.6 0.8 fusion
  135.4 2.5 %reshape.231 = f32[6,64,3,4,64]{4,3,2,1,0:T(4,128)} reshape(f32[384,768]{1,0:T(8,128)S(1)} %fusion) | data formatting | bytes 2359296 | tf_op jit(solution)/shard_map/reshape | solution.py:303
  137.8 1.3 slice.146
  139.1 1.5 fusion.61
  140.6 1.0 copy.135
  142.1 1.6 fusion.11
  143.7 1.8 fusion.18
  145.8 1.0 reshape.232
  146.7 2.2 fusion.2
  148.9 2.5 %reshape.229 = f32[6,64,3,4,64]{4,3,2,1,0:T(4,128)} reshape(f32[384,768]{1,0:T(8,128)S(1)} %fusion.2) | data formatting | bytes 2359296 | tf_op jit(solution)/shard_map/reshape | solution.py:303
  151.4 1.3 slice.142
  152.7 1.5 fusion.64
  154.1 1.0 copy.134
  155.7 1.5 fusion.12
  157.2 1.6 fusion.17
  159.4 2.3 convolution_convert_fusion.1
  161.7 3.4 %fusion.4 = f32[384,768]{1,0:T(8,128)} fusion(bf16[384,1024]{1,0:T(8,128)(2,1)S(1)} %bitcast.153, bf16[1024,1024]{1,0:T(8,128)(2,1)} %get-tuple-element.13), kind=kOutput, calls=%fused_computation.8 | convolution fusion | flops 603979776 | bytes 3538944 | tf_op jit(solution)/shard_map/dot_general | solution.py:260
  165.1 0.8 fusion.6
  165.9 2.5 %reshape.225 = f32[6,64,3,4,64]{4,3,2,1,0:T(4,128)} reshape(f32[384,768]{1,0:T(8,128)S(1)} %fusion.6) | data formatting | bytes 2359296 | tf_op jit(solution)/shard_map/reshape | solution.py:303
  168.3 1.3 slice.134
  169.6 1.5 fusion.62
  171.1 1.0 copy.132
  172.6 1.6 fusion.14
  174.2 2.6 %fusion.15 = bf16[6,64,4,64]{1,3,2,0:T(8,128)(2,1)} fusion(f32[6,4,64,64]{2,3,1,0:T(8,128)} %fusion.14, bf16[6,64,1,4,64]{1,4,3,0,2:T(8,128)(2,1)S(1)} %copy-done.10), kind=kOutput, calls=%fused_computation.37 | convolution fusion | flops 12879423 | bytes 786432 | tf_op jit(solution)/shard_map/bhqk,bkhd->bqhd/dot_general | solution.py:310
  176.8 1.3 copy.99
  178.5 2.3 convolution_convert_fusion.3
  180.8 2.5 %reshape.227 = f32[6,64,3,4,64]{4,3,2,1,0:T(4,128)} reshape(f32[384,768]{1,0:T(8,128)S(1)} %copy-done.4) | data formatting | bytes 2359296 | tf_op jit(solution)/shard_map/reshape | solution.py:303
  183.3 1.3 slice.138
  184.5 1.5 fusion.63
  186.0 1.0 copy.133
  187.6 1.6 fusion.13
  189.1 1.7 fusion.16
  191.3 1.4 convolution_convert_fusion.2
  192.8 2.4 %fusion.66 = (f32[384]{0:T(512)S(1)}, f32[384,1024]{1,0:T(8,128)S(1)}) fusion(bf16[384,256]{1,0:T(8,128)(2,1)S(1)} %copy-done.5, bf16[3,4,1024,1024]{3,2,1,0:T(8,128)(2,1)} %get-tuple-element.7.up_ref.down_ref, bf16[384,1024]{1,0:T(8,128)(2,1)} %convolution_convert_fusion.1, bf16[384,1024]{1,0:T(8,128)(2,1)S(1)} %convolution_convert_fusion.2, ...), kind=kOutput, calls=%fused_computation.145 | convolution fusion | flops 205651584 | bytes 5441024 | tf_op jit(solution)/shard_map/dot_general | solution.py:264
  195.9 1.2 multiply_convert_fusion.normed_ref
  197.1 11.9 %feed_forward.1 = f32[384,1024]{1,0:T(8,128)} custom-call(bf16[384,1024]{1,0:T(8,128)(2,1)} %multiply_convert_fusion.normed_ref, bf16[3,4,1024,1024]{3,2,1,0:T(8,128)(2,1)} %get-tuple-element.7.up_ref.down_ref, bf16[3,4,1024,1024]{3,2,1,0:T(8,128)(2,1)} %get-tuple-element.7.up_ref.down_ref, f32[384,1024]{1,0:T(8,128)} %copy-done.1), custom_call_target="tpu_custom_call" | custom-call | tf_op jit(solution)/shard_map/feed_forward/pallas_call | solution.py:238
  209.0 1.6 reduce_sum.232
  211.5 0.7 multiply_convert_fusion.19.own_ref
  212.2 15.1 %share_units.1 = bf16[32,6,768]{2,1,0:T(8,128)(2,1)} custom-call(bf16[6,768]{1,0:T(8,128)(2,1)} %multiply_convert_fusion.19.own_ref), custom_call_target="tpu_custom_call" | custom-call | tf_op jit(solution)/shard_map/share_units/pallas_call | solution.py:209
  227.3 1.1 reshape.234
  229.1 0.7 maximum_bitcast_fusion.1.own_ref
  229.8 9.6 %spread_stats.1 = f32[32,3,6]{2,1,0:T(4,128)} custom-call(f32[32,3,6]{2,1,0:T(4,128)} %maximum_bitcast_fusion.1.own_ref), custom_call_target="tpu_custom_call" | custom-call | tf_op jit(solution)/shard_map/spread_stats/pallas_call | solution.py:209
  239.4 1.0 fusion.65
  (91 shorter events, 8.5 us)
Async XLA Ops:
  0.0 211.0 %copy-start = (bf16[1024,768]{1,0:T(8,128)(2,1)S(1)}, bf16[1024,768]{1,0:T(8,128)(2,1)}, u32[]{:S(2)}) copy-start(bf16[1024,768]{1,0:T(8,128)(2,1)} %param.22) | copy-start | bytes 4718596
  0.0 3.9 %copy-start.12 = (bf16[1024,128]{1,0:T(8,128)(2,1)S(1)}, bf16[1024,128]{1,0:T(8,128)(2,1)}, u32[]{:S(2)}) copy-start(bf16[1024,128]{1,0:T(8,128)(2,1)} %param.20) | copy-start | bytes 786436
  0.0 3.4 %copy-start.16 = (bf16[256,128]{1,0:T(8,128)(2,1)S(1)}, bf16[256,128]{1,0:T(8,128)(2,1)}, u32[]{:S(2)}) copy-start(bf16[256,128]{1,0:T(8,128)(2,1)} %param.17) | copy-start | bytes 196612
  0.0 3.6 %copy-start.14 = (bf16[128,3,256]{2,0,1:T(8,128)(2,1)S(1)}, bf16[128,3,256]{2,0,1:T(8,128)(2,1)}, u32[]{:S(2)}) copy-start(bf16[128,3,256]{2,0,1:T(8,128)(2,1)} %param.15) | copy-start | bytes 589828
  1.9 2.2 copy-start.13
  3.7 1.4 copy-start.2
  3.8 1.4 copy-start.17
  5.5 129.1 %copy-start.6 = (bf16[6,64,1024]{2,1,0:T(8,128)(2,1)}, bf16[6,64,1024]{2,1,0:T(8,128)(2,1)S(1)}, u32[]{:S(2)}) copy-start(bf16[6,64,1024]{2,1,0:T(8,128)(2,1)S(1)} %multiply_convert_fusion.1) | copy-start | bytes 2359300
  143.7 3.1 %copy-start.7 = (bf16[6,64,1024]{2,1,0:T(8,128)(2,1)S(1)}, bf16[6,64,1024]{2,1,0:T(8,128)(2,1)}, u32[]{:S(2)}) copy-start(bf16[6,64,1024]{2,1,0:T(8,128)(2,1)} %copy-done.6) | copy-start | bytes 2359300
  155.6 1.6 copy-start.9
  158.8 2.9 %copy-start.8 = (bf16[6,64,1024]{2,1,0:T(8,128)(2,1)S(1)}, bf16[6,64,1024]{2,1,0:T(8,128)(2,1)}, u32[]{:S(2)}) copy-start(bf16[6,64,1024]{2,1,0:T(8,128)(2,1)} %copy-done.6) | copy-start | bytes 2359300
  161.7 3.4 %copy-start.3 = (bf16[1024,1024]{1,0:T(8,128)(2,1)S(1)}, bf16[1024,1024]{1,0:T(8,128)(2,1)}, u32[]{:S(2)}) copy-start(bf16[1024,1024]{1,0:T(8,128)(2,1)} %get-tuple-element.14) | copy-start | bytes 6291460
  172.6 1.6 copy-start.10
  176.8 4.0 %copy-start.4 = (f32[384,768]{1,0:T(8,128)S(1)}, f32[384,768]{1,0:T(8,128)}, u32[]{:S(2)}) copy-start(f32[384,768]{1,0:T(8,128)} %fusion.4) | copy-start | bytes 3538948
  187.5 1.6 copy-start.11
  190.8 2.0 copy-start.5
  195.2 1.9 copy-start.1
  195.3 0.7 copy-start.18
  209.0 1.9 copy-start.19
  210.6 17.7 %copy-start.15 = (bf16[96,768]{1,0:T(8,128)(2,1)S(1)}, bf16[96,768]{1,0:T(8,128)(2,1)}, u32[]{:S(2)}) copy-start(bf16[96,768]{1,0:T(8,128)(2,1)} %param.23) | copy-start | bytes 442372
  211.0 17.6 %copy-start.20 = (s32[192]{0:T(256)S(1)}, s32[192]{0:T(256)}, u32[]{:S(2)}) copy-start(s32[192]{0:T(256)} %param.24) | copy-start | bytes 2308
  211.0 17.6 %copy-start.21 = (s32[96]{0:T(128)S(1)}, s32[96]{0:T(128)}, u32[]{:S(2)}) copy-start(s32[96]{0:T(128)} %iota_add_fusion) | copy-start | bytes 1156
  211.0 29.4 %copy-start.22 = (f32[6]{0:T(128)S(1)}, f32[6]{0:T(128)}, u32[]{:S(2)}) copy-start(f32[6]{0:T(128)} %param.25) | copy-start | bytes 76

commit v3 on v2

--- a/solution.py
+++ b/solution.py
@@ -221,6 +221,58 @@
     )(own)
 
 
+def attention_kernel(images, heads, scale_ref, normed_ref, weight_ref, residual_ref, total_ref, head_ref):
+    group = pl.program_id(0)
+
+    @pl.when(group == 0)
+    def _():
+        total_ref[...] = residual_ref[...]
+
+    tokens, width = head_ref.shape
+    head_width = width // heads
+    joint = dot(normed_ref[...], weight_ref[:, : 3 * width])
+
+    def rows_of(part, head):
+        first = part * width + head * head_width
+        return joint[:, first : first + head_width]
+
+    def by_image(values):
+        return values.astype(jnp.bfloat16).reshape(images, tokens // images, head_width)
+
+    for head in range(heads):
+        queries = by_image(unit_rows(rows_of(0, head)))
+        key_rows = by_image(unit_rows(rows_of(1, head)))
+        value_rows = by_image(rows_of(2, head))
+        scores = jnp.einsum("bqd,bkd->bqk", queries, key_rows, preferred_element_type=jnp.float32)
+        exponent = jnp.exp(scores * scale_ref[group, head])
+        attention = (exponent / jnp.sum(exponent, axis=-1, keepdims=True)).astype(jnp.bfloat16)
+        mixed = jnp.einsum("bqk,bkd->bqd", attention, value_rows, preferred_element_type=jnp.float32)
+        head_ref[:, head * head_width : (head + 1) * head_width] = mixed.astype(jnp.bfloat16).reshape(
+            tokens, head_width
+        )
+    total_ref[...] += grouped(dot_t(head_ref[...], weight_ref[:, 3 * width :]))
+
+
+def attend(scales, normed, full, residual, images, width):
+    _, groups, features, columns = full.shape
+    whole = pl.BlockSpec(normed.shape, lambda m: (0, 0))
+    return pl.pallas_call(
+        functools.partial(attention_kernel, images, scales.shape[1]),
+        grid=(groups,),
+        out_shape=jax.ShapeDtypeStruct(residual.shape, jnp.float32),
+        in_specs=[
+            pl.BlockSpec(memory_space=pltpu.SMEM),
+            whole,
+            pl.BlockSpec((None, None, features, columns), lambda m: (0, m, 0, 0)),
+            whole,
+        ],
+        out_specs=whole,
+        scratch_shapes=[pltpu.VMEM((normed.shape[0], width), jnp.bfloat16)],
+        compiler_params=pltpu.CompilerParams(dimension_semantics=("arbitrary",)),
+        name="attend",
+    )(scales, normed, full, residual)
+
+
 def feed_kernel(normed_ref, up_ref, down_ref, residual_ref, total_ref):
     @pl.when(pl.program_id(0) == 0)
     def _():
@@ -286,9 +338,7 @@
     n_dp, n_mp = lax.axis_size("dp"), lax.axis_size("mp")
     own_images, patch_count, features = patches.shape
     rows = joint_weight.shape[0]
-    local_heads = head_scale.shape[0]
     width = joint_weight.shape[2]
-    head_width = width // local_heads
     tokens = own_images * patch_count
 
     attention_part = jnp.concatenate([joint_weight.reshape(rows, 3 * width), output_weight.T], axis=1)
@@ -297,20 +347,7 @@
 
     residual = patches.astype(jnp.float32).reshape(tokens, features)
     normed_first = layer_norm(residual, gain_first).astype(jnp.bfloat16)
-    residual_two = residual
-    for m in range(n_mp):
-        joint = dot(normed_first, full[0, m])[:, : 3 * width]
-        joint = joint.reshape(own_images, patch_count, 3, local_heads, head_width)
-        queries = unit_rows(joint[:, :, 0]).astype(jnp.bfloat16)
-        key_rows = unit_rows(joint[:, :, 1]).astype(jnp.bfloat16)
-        value_rows = joint[:, :, 2].astype(jnp.bfloat16)
-        scores = jnp.einsum("bqhd,bkhd->bhqk", queries, key_rows, preferred_element_type=jnp.float32)
-        exponent = jnp.exp(scores * scales[m, 0][None, :, None, None])
-        attention = (exponent / jnp.sum(exponent, axis=-1, keepdims=True)).astype(jnp.bfloat16)
-        head_out = jnp.einsum(
-            "bhqk,bkhd->bqhd", attention, value_rows, preferred_element_type=jnp.float32
-        ).astype(jnp.bfloat16).reshape(tokens, width)
-        residual_two = residual_two + grouped(dot_t(head_out, full[0, m, :, 3 * width :]))
+    residual_two = attend(scales[:, 0], normed_first, full, residual, own_images, width)
     normed_second = layer_norm(residual_two, gain_second).astype(jnp.bfloat16)
     total = feed_forward(normed_second, full, residual_two)
     pooled = jnp.sum(total.reshape(own_images, patch_count, features), axis=1) / patch_count

time: 242 us -> 197 us (0.81)
  local copies, waits for them, and re-layouts: 37.4 us -> 4.25 us
  matrix products: 30.4 us -> 0.72 us
  Pallas kernels: 159 us -> 180 us
    pallas_call x0 -> x1, Pallas kernels: none -> 20.4 us  [attend(): pl.pallas_call(functools.partial(attention_kernel, images, scales.shape[1...]
    dot_general x8 -> x0, matrix products: 14 us -> none  [the longest x4 7.8 us: shards(): jnp.einsum('bhqk,bkhd->bqhd', attention, value_rows, preferred_element_ty...]
    reshape x8 -> x0, local copies, waits for them, and re-layouts: 11.7 us -> none  [the longest x4 9.88 us: shards(): joint = joint.reshape(own_images, patch_count, 3, local_heads, head_width)]
    slice x8 -> x0, local copies, waits for them, and re-layouts: 11 us -> none  [the longest x4 5.9 us: shards(): key_rows = unit_rows(joint[:, :, 1]).astype(jnp.bfloat16)]
    dot_general x5 -> x1, matrix products: 8.81 us -> 0.26 us  [dot_t(): lax.dot_general(left, right, (((1,), (1,)), ((), ())), preferred_element_...]
    dot_general x5 -> x1, matrix products: 7.58 us -> 0.47 us  [dot(): return jnp.dot(left, right, preferred_element_type=jnp.float32)]
    squeeze x1 -> x0, local copies, waits for them, and re-layouts: 5.68 us -> none  [shards(): joint = dot(normed_first, full[0, m])[:, :3 * width]]
    unnamed x53 -> x25, local copies, waits for them, and re-layouts: 4.85 us -> 2.55 us
where the time goes in v3:
time: 197 us
  Pallas kernels  180 us (91%)
  other arithmetic  12.3 us (6%)
  local copies, waits for them, and re-layouts  4.25 us (2%)
    pallas_call x1, Pallas kernels, gather_weights(): pl.pallas_call(functools.partial(gather_kernel, n_mp), out_shape=(jax.Sha...  123 us
    pallas_call x2, Pallas kernels, exchange(): pl.pallas_call(functools.partial(exchange_kernel, n_dp, n_mp, spread), ou...  24.7 us
    pallas_call x1, Pallas kernels, attend(): pl.pallas_call(functools.partial(attention_kernel, images, scales.shape[1...  20.4 us
    pallas_call x1, Pallas kernels, feed_forward(): pl.pallas_call(feed_kernel, grid=(groups,), out_shape=jax.ShapeDtypeStruc...  11.9 us

profile of v3, /device:TPU:0, one launch (start us, length us, event | category | flops | bytes accessed | tf_op | source)
XLA Modules:
  0.0 197.0 jit_solution(3304848896426388937)
XLA Ops:
  0.0 0.0 copy-start
  0.0 1.2 copy.35
  1.2 0.2 copy.37
  1.4 0.9 copy.36
  2.4 0.0 copy-done.3
  2.4 0.0 copy-start.2
  2.4 0.1 copy.38
  2.5 0.0 copy-done.4
  2.6 1.0 pad_maximum_fusion.own_ref
  3.6 122.5 %gather_weights.1 = (bf16[3,4,1024,1024]{3,2,1,0:T(8,128)(2,1)}, f32[4,1,4]{2,1,0:T(1,128)}) custom-call(bf16[3,128,1024]{2,1,0:T(8,128)(2,1)} %pad_maximum_fusion.own_ref, f32[1,4]{1,0:T(1,128)} %bitcast.39), custom_call_target="tpu_custom_call" | custom-call | tf_op jit(solution)/shard_map/gather_weights/pallas_call | solution.py:140
  126.1 0.0 copy-done.2
  126.1 0.2 convert_reduce_fusion
  126.3 0.3 multiply_reduce_fusion.1
  126.6 0.1 rsqrt.36
  126.7 0.1 div.27
  126.8 0.0 copy-done.6
  126.8 1.2 multiply_convert_fusion.1.normed_ref
  128.0 1.4 bitcast_convert_fusion.residual_ref
  129.4 20.4 %attend.1.residual_ref = f32[384,1024]{1,0:T(8,128)} custom-call(f32[4,4]{1,0:T(4,128)} %bitcast.38, bf16[384,1024]{1,0:T(8,128)(2,1)} %multiply_convert_fusion.1.normed_ref, bf16[3,4,1024,1024]{3,2,1,0:T(8,128)(2,1)} %get-tuple-element.8.weight_ref.up_ref.down_ref, f32[384,1024]{1,0:T(8,128)} %bitcast_convert_fusion.residual_ref), custom_call_target="tpu_custom_call" | custom-call | tf_op jit(solution)/shard_map/attend/pallas_call | solution.py:259
  149.8 1.7 reduce_sum.110
  151.5 0.2 copy-done.1
  151.6 0.3 multiply_reduce_fusion
  152.0 0.0 copy-done.7
  152.0 1.2 multiply_convert_fusion.normed_ref
  153.1 11.9 %feed_forward.1 = f32[384,1024]{1,0:T(8,128)} custom-call(bf16[384,1024]{1,0:T(8,128)(2,1)} %multiply_convert_fusion.normed_ref, bf16[3,4,1024,1024]{3,2,1,0:T(8,128)(2,1)} %get-tuple-element.8.weight_ref.up_ref.down_ref, bf16[3,4,1024,1024]{3,2,1,0:T(8,128)(2,1)} %get-tuple-element.8.weight_ref.up_ref.down_ref, f32[384,1024]{1,0:T(8,128)} %attend.1.residual_ref), custom_call_target="tpu_custom_call" | custom-call | tf_op jit(solution)/shard_map/feed_forward/pallas_call | solution.py:290
  165.1 1.6 reduce_sum.112
  166.7 0.0 copy-start.5
  166.7 0.1 multiply_reduce_fusion.3
  166.8 0.2 multiply_reduce_fusion.2
  167.0 0.0 copy-done
  167.0 0.0 copy-done.8
  167.0 0.0 copy-start.9
  167.0 0.0 copy-start.10
  167.0 0.5 multiply_reduce_fusion.4
  167.5 0.7 multiply_convert_fusion.3.own_ref
  168.2 15.1 %share_units.1 = bf16[32,6,768]{2,1,0:T(8,128)(2,1)} custom-call(bf16[6,768]{1,0:T(8,128)(2,1)} %multiply_convert_fusion.3.own_ref), custom_call_target="tpu_custom_call" | custom-call | tf_op jit(solution)/shard_map/share_units/pallas_call | solution.py:209
  183.3 1.1 reshape.90
  184.4 0.0 copy-done.5
  184.4 0.3 fusion.7
  184.7 0.0 copy-done.9
  184.7 0.1 exponential_reduce_fusion
  184.8 0.1 stack.29
  184.9 0.1 stack.30
  185.0 0.1 stack.28
  185.1 0.7 maximum_bitcast_fusion.1.own_ref
  185.8 9.6 %spread_stats.1 = f32[32,3,6]{2,1,0:T(4,128)} custom-call(f32[32,3,6]{2,1,0:T(4,128)} %maximum_bitcast_fusion.1.own_ref), custom_call_target="tpu_custom_call" | custom-call | tf_op jit(solution)/shard_map/spread_stats/pallas_call | solution.py:209
  195.4 1.0 fusion.6
  196.5 0.5 subtract_subtract_fusion
  (18 shorter events, 0.1 us)
Async XLA Ops:
  0.0 167.0 %copy-start = (bf16[1024,768]{1,0:T(8,128)(2,1)S(1)}, bf16[1024,768]{1,0:T(8,128)(2,1)}, u32[]{:S(2)}) copy-start(bf16[1024,768]{1,0:T(8,128)(2,1)} %param.22) | copy-start | bytes 4718596
  0.0 2.4 %copy-start.3 = (bf16[1024,128]{1,0:T(8,128)(2,1)S(1)}, bf16[1024,128]{1,0:T(8,128)(2,1)}, u32[]{:S(2)}) copy-start(bf16[1024,128]{1,0:T(8,128)(2,1)} %param.20) | copy-start | bytes 786436
  0.0 2.5 %copy-start.4 = (bf16[128,1024]{1,0:T(8,128)(2,1)S(1)}, bf16[128,1024]{1,0:T(8,128)(2,1)}, u32[]{:S(2)}) copy-start(bf16[128,1024]{1,0:T(8,128)(2,1)} %param.19) | copy-start | bytes 786436
  2.4 123.7 %copy-start.2 = (bf16[6,64,1024]{2,1,0:T(8,128)(2,1)S(1)}, bf16[6,64,1024]{2,1,0:T(8,128)(2,1)}, u32[]{:S(2)}) copy-start(bf16[6,64,1024]{2,1,0:T(8,128)(2,1)} %param.13) | copy-start | bytes 2359300
  3.6 123.2 %copy-start.6 = (f32[1024]{0:T(1024)S(1)}, f32[1024]{0:T(1024)}, u32[]{:S(2)}) copy-start(f32[1024]{0:T(1024)} %param.14) | copy-start | bytes 12292
  149.8 1.9 copy-start.1
  149.8 2.2 %copy-start.7 = (f32[1024]{0:T(1024)S(1)}, f32[1024]{0:T(1024)}, u32[]{:S(2)}) copy-start(f32[1024]{0:T(1024)} %param.18) | copy-start | bytes 12292
  165.1 1.9 copy-start.8
  166.7 17.8 %copy-start.5 = (bf16[96,768]{1,0:T(8,128)(2,1)S(1)}, bf16[96,768]{1,0:T(8,128)(2,1)}, u32[]{:S(2)}) copy-start(bf16[96,768]{1,0:T(8,128)(2,1)} %param.23) | copy-start | bytes 442372
  167.0 17.7 %copy-start.9 = (s32[192]{0:T(256)S(1)}, s32[192]{0:T(256)}, u32[]{:S(2)}) copy-start(s32[192]{0:T(256)} %param.24) | copy-start | bytes 2308
  167.0 29.5 %copy-start.10 = (f32[6]{0:T(128)S(1)}, f32[6]{0:T(128)}, u32[]{:S(2)}) copy-start(f32[6]{0:T(128)} %param.25) | copy-start | bytes 76
